TPU v7x, 512 devices: a whole 4x8x8 slice. The times are simulated.
512 devices in a mesh: band: 16 (over y, z_lo), ga: 32 (over x, z_hi, core).
Axes of the slice: x: 4, y: 8, z: 8 (z_hi: 4, z_lo: 2; z = z_hi * 2 + z_lo), core: 2. Of those that a mesh axis runs over, the one named last changes fastest.
Arguments:
- orbitals: bfloat16 [32768, 4096], P('ga', 'band'), may hold values from -6 to 6
Outputs:
- margin: float32 [4096, 4096], P('band', 'ga')
- corrected: bfloat16 [32768, 4096], P('ga', 'band')
All inputs are finite; a program needn't handle non-finite values.
Results may differ from a plain program's by a relative error of at most 0.0056.
Values may be sent and summed in bfloat16 or wider, within the bound.
A program may use at most 64 MiB of HBM per device.

v0:
```python
import jax
import jax.numpy as jnp
from jax import lax
from jax.sharding import Mesh
from jax.sharding import PartitionSpec as P

BAND = ("band_0", "band_1")


def whole_of(value, axes, dim):
    if not axes:
        return value
    nearer = lax.all_gather(value, axes[-1], axis=dim, tiled=True)
    return whole_of(nearer, axes[:-1], dim)


def split_up(value, dim, count):
    before, after = (value.shape[:dim], value.shape[dim + 1 :])
    return jnp.moveaxis(value.reshape(*before, count, -1, *after), dim, 0)


def sum_at_owner(value, axis, dim):
    blocks = split_up(value, dim, lax.axis_size(axis))
    arrived = lax.all_to_all(blocks, axis, split_axis=0, concat_axis=0, tiled=True)
    return arrived.astype(jnp.float32).sum(axis=0)


def in_order(blocks, dim):
    dims = list(blocks.shape[1:])
    dims[dim] *= blocks.shape[0]
    return jnp.moveaxis(blocks, 0, dim).reshape(dims)


def sent_to_all(value, axis):
    count = lax.axis_size(axis)
    return lax.all_to_all(
        jnp.broadcast_to(value[None], (count, *value.shape)), axis, 0, 0, tiled=True
    )


def gathered_copies(value, axis, dim):
    return in_order(sent_to_all(value, axis), dim)


def identity_block(rows, cols, row_start, col_start):
    row_index = row_start + lax.iota(jnp.int32, rows)
    col_index = col_start + lax.iota(jnp.int32, cols)
    return (row_index[:, None] == col_index[None, :]).astype(jnp.float32)


def shards(orbitals):
    own_coeffs = orbitals.shape[0]
    own_bands = orbitals.shape[1]
    all_bands = own_bands * lax.axis_size(BAND)
    all_coeffs = own_coeffs * lax.axis_size("ga")
    col_width = all_bands // lax.axis_size("ga")
    row_start = lax.axis_index(BAND) * own_bands
    col_start = lax.axis_index("ga") * col_width
    everyone = whole_of(orbitals, BAND, 1)
    partial_value = lax.dot_general(
        orbitals, everyone, (((0,), (0,)), ((), ())), preferred_element_type=jnp.float32
    )
    unit_block = identity_block(own_bands, col_width, row_start, col_start)
    margin_block = sum_at_owner(partial_value.astype(jnp.bfloat16), "ga", 1) / all_coeffs
    deviation_block = margin_block - unit_block
    deviation_rows = lax.all_gather(
        deviation_block.astype(jnp.bfloat16), "ga", axis=1, tiled=True
    ).astype(deviation_block.dtype)
    deviation_cols = gathered_copies(deviation_block.astype(jnp.bfloat16), BAND, 0).astype(
        deviation_block.dtype
    )
    square = jnp.dot(
        deviation_rows,
        deviation_cols,
        precision=lax.Precision.HIGHEST,
        preferred_element_type=jnp.float32,
    )
    fix_block = (unit_block - 0.5 * deviation_block + 0.375 * square).astype(jnp.bfloat16)
    fix_rows = gathered_copies(fix_block, "ga", 1)
    corrected = lax.dot_general(
        everyone, fix_rows, (((1,), (1,)), ((), ())), preferred_element_type=jnp.float32
    )
    return (margin_block, corrected.astype(jnp.bfloat16))


def solution(mesh):
    finer = Mesh(mesh.devices.reshape(8, 2, mesh.shape["ga"]), ("band_0", "band_1", "ga"))
    placed = (P("ga", BAND),)
    return jax.shard_map(
        shards,
        mesh=finer,
        in_specs=placed,
        out_specs=(P(BAND, "ga"), P("ga", BAND)),
        check_vma=False,
    )
```

profile of v0, /device:TPU:1, one launch (start us, length us, event | category | flops | bytes accessed | tf_op | source)
XLA Modules:
  0.0 347.4 jit_solution(5040010379792881687)
XLA Ops:
  7.2 0.0 all-gather.4.cloned.1.call-start
  7.2 0.7 all-gather.4.cloned.1.call-update
  7.9 0.0 all-gather.6.cloned.1.call-start
  7.9 36.7 %all-gather.4.cloned.1.call-done = bf16[1024,512]{1,0:T(8,128)(2,1)} async-done(((bf16[1024,256]{1,0:T(8,128)(2,1)}), bf16[1024,512]{1,0:T(8,128)(2,1)}) %all-gather.4.cloned.1.call-update) | async-done | bytes 1048592 | tf_op jit(solution)/shard_map/all_gather | solution.py:13
  44.7 0.0 all-gather.6.cloned.1.call-update
  44.7 98.9 %all-gather.6.cloned.1.call-done = bf16[1024,4096]{1,0:T(8,128)(2,1)} async-done(((bf16[1024,512]{1,0:T(8,128)(2,1)}), bf16[1024,4096]{1,0:T(8,128)(2,1)}) %all-gather.6.cloned.1.call-update) | async-done | bytes 8388624 | tf_op jit(solution)/shard_map/all_gather | solution.py:13
  143.6 6.0 %fusion = bf16[32,32,8,128]{3,2,1,0:T(8,128)(2,1)S(1)} fusion(bf16[1024,256]{1,0:T(8,128)(2,1)} %param.1, bf16[1024,4096]{1,0:T(8,128)(2,1)} %all-gather.6.cloned.1.call-done), kind=kOutput, calls=%fused_computation.3 | convolution fusion | flops 2148532224 | bytes 11010048 | tf_op jit(solution)/shard_map/dot_general | solution.py:60
  149.6 1.9 copy.11
  151.5 10.8 %all-to-all-start = ((bf16[32,256,128]{2,1,0:T(8,128)(2,1)}), bf16[32,256,128]{2,1,0:T(8,128)(2,1)S(1)}, u32[]{:S(2)}, u32[]{:S(2)}) async-start(bf16[32,256,128]{2,1,0:T(8,128)(2,1)} %bitcast.20), calls=%async_computation | async-start | bytes 4194304 | tf_op jit(solution)/shard_map/all_to_all | solution.py:24
  162.3 0.0 all-gather.8.cloned.1.call-start
  162.4 51.7 %all-to-all-done = bf16[32,256,128]{2,1,0:T(8,128)(2,1)S(1)} async-done(((bf16[32,256,128]{2,1,0:T(8,128)(2,1)}), bf16[32,256,128]{2,1,0:T(8,128)(2,1)S(1)}, u32[]{:S(2)}, u32[]{:S(2)}) %all-to-all-start) | async-done | bytes 2097184 | tf_op jit(solution)/shard_map/all_to_all | solution.py:24
  214.0 0.3 convert_reduce_fusion
  214.3 0.7 fusion.4
  215.1 0.0 copy-start
  215.1 0.0 all-gather.8.cloned.1.call-update
  215.1 1.1 broadcast_in_dim.4
  216.2 30.9 %all_to_all.15 = bf16[16,256,128]{2,1,0:T(8,128)(2,1)S(1)} all-to-all(bf16[16,256,128]{2,1,0:T(8,128)(2,1)S(1)} %broadcast_in_dim.4), channel_id=1, replica_groups=mesh['band_0'=8,'band_1'=2,'ga'=32] {'band_0','band_1'}, dimensions={0} | all-to-all | bytes 2097152 | tf_op jit(solution)/shard_map/all_to_all | solution.py:36
  247.1 27.0 %all-gather.8.cloned.1.call-done = bf16[256,4096]{1,0:T(8,128)(2,1)} async-done(((bf16[256,128]{1,0:T(8,128)(2,1)}), bf16[256,4096]{1,0:T(8,128)(2,1)}) %all-gather.8.cloned.1.call-update) | async-done | bytes 2097168 | tf_op jit(solution)/shard_map/all_gather | solution.py:66
  274.1 2.3 fusion.3
  276.4 0.0 copy-done
  276.4 0.1 copy.7
  276.5 0.2 broadcast_in_dim.5
  276.8 57.4 %all_to_all.16 = bf16[32,256,128]{1,2,0:T(8,128)(2,1)S(1)} all-to-all(bf16[32,256,128]{1,2,0:T(8,128)(2,1)S(1)} %broadcast_in_dim.5), channel_id=1, replica_groups=mesh['band_0'=8,'band_1'=2,'ga'=32] {'ga'}, dimensions={0} | all-to-all | bytes 4194304 | tf_op jit(solution)/shard_map/all_to_all | solution.py:36
  334.1 5.8 %fusion.1 = bf16[1024,256]{0,1:T(8,128)(2,1)S(1)} fusion(bf16[256,4096]{0,1:T(8,128)(2,1)S(1)} %bitcast.22, bf16[1024,4096]{1,0:T(8,128)(2,1)} %all-gather.6.cloned.1.call-done), kind=kOutput, calls=%fused_computation.5 | convolution fusion | flops 2147745792 | bytes 11010048 | tf_op jit(solution)/shard_map/dot_general | solution.py:80
  339.9 1.0 copy.8
  (2 shorter events, 0.0 us)
Async XLA Ops:
  7.2 37.5 %all-gather.4.cloned.1.call-start = ((), (), s32[]{:S(2)}) async-start(), calls=%async_computation.3 | async-start | bytes 1572864 | tf_op jit(solution)/shard_map/all_gather | solution.py:13
  7.9 135.7 %all-gather.6.cloned.1.call-start = ((), (), s32[]{:S(2)}) async-start(), calls=%async_computation.4 | async-start | bytes 9437184 | tf_op jit(solution)/shard_map/all_gather | solution.py:13
  151.5 62.5 %all-to-all-start = ((bf16[32,256,128]{2,1,0:T(8,128)(2,1)}), bf16[32,256,128]{2,1,0:T(8,128)(2,1)S(1)}, u32[]{:S(2)}, u32[]{:S(2)}) async-start(bf16[32,256,128]{2,1,0:T(8,128)(2,1)} %bitcast.20), calls=%async_computation | async-start | bytes 4194304 | tf_op jit(solution)/shard_map/all_to_all | solution.py:24
  162.3 111.8 %all-gather.8.cloned.1.call-start = ((), (), s32[]{:S(2)}) async-start(), calls=%async_computation.5 | async-start | bytes 2162688 | tf_op jit(solution)/shard_map/all_gather | solution.py:66
  215.1 61.4 %copy-start = (f32[256,128]{1,0:T(8,128)}, f32[256,128]{1,0:T(8,128)S(1)}, u32[]{:S(2)}) copy-start(f32[256,128]{1,0:T(8,128)S(1)} %get-tuple-element.9) | copy-start | bytes 393220
Sparse Core Ops, SparseCore 0:
  10.0 34.5 all-gather.3
  46.8 96.7 all-gather.5
  215.2 58.8 all-gather.7
where the time goes:
time: 348 us; the launch traced here: 347 us
  waiting for transfers between devices  215 us (62%)
  blocking collectives  88.3 us (25%)
  matrix products  14 us (4%)
  between operations  13.8 us (4%)
  starting transfers between devices  10.9 us (3%)
  local copies, waits for them, and re-layouts  4.35 us (1%)
    all_gather x2, waiting for transfers between devices, whole_of(): nearer = lax.all_gather(value, axes[-1], axis=dim, tiled=True)  136 us
    all_to_all x2, blocking collectives, sent_to_all(): lax.all_to_all(jnp.broadcast_to(value[None], (count, *value.shape)), axis...  88.3 us
    all_to_all x1, waiting for transfers between devices, sum_at_owner(): lax.all_to_all(blocks, axis, split_axis=0, concat_axis=0, tiled=True)  51.7 us
    all_gather x1, waiting for transfers between devices, shards(): lax.all_gather(deviation_block.astype(jnp.bfloat16), 'ga', axis=1, tiled=...  27 us
    all_to_all x1, starting transfers between devices, sum_at_owner(): lax.all_to_all(blocks, axis, split_axis=0, concat_axis=0, tiled=True)  10.8 us
  transfers between devices with their start and end apart: 4, of which 4 were waited for; matrix products, arithmetic and copies ran while one was open for 0% of the time, Pallas kernels for 0%

commit v1 on v0

--- a/solution.py
+++ b/solution.py
@@ -63,8 +63,11 @@
     unit_block = identity_block(own_bands, col_width, row_start, col_start)
     margin_block = sum_at_owner(partial_value.astype(jnp.bfloat16), "ga", 1) / all_coeffs
     deviation_block = margin_block - unit_block
-    deviation_rows = lax.all_gather(
-        deviation_block.astype(jnp.bfloat16), "ga", axis=1, tiled=True
+    deviation_rows = jnp.concatenate(
+        lax.all_to_all(
+            jnp.stack([deviation_block.astype(jnp.bfloat16)] * lax.axis_size("ga")), "ga", 0, 0
+        ),
+        axis=1,
     ).astype(deviation_block.dtype)
     deviation_cols = gathered_copies(deviation_block.astype(jnp.bfloat16), BAND, 0).astype(
         deviation_block.dtype

time: 348 us -> 377 us (1.083)
  blocking collectives: 88.3 us -> 117 us
  starting transfers between devices: 10.9 us -> 15.2 us
    all_to_all x0 -> x1, blocking collectives: none -> 59.9 us  [shards(): lax.all_to_all(jnp.stack([deviation_block.astype(jnp.bfloat16)] * lax.axi...]
    all_to_all x2 -> x1, blocking collectives: 88.3 us -> 57.1 us  [sent_to_all(): lax.all_to_all(jnp.broadcast_to(value[None], (count, *value.shape)), axis...]
    all_gather x1 -> x0, waiting for transfers between devices: 27 us -> none  [shards(): lax.all_gather(deviation_block.astype(jnp.bfloat16), 'ga', axis=1, tiled=...]
    all_to_all x0 -> x1, waiting for transfers between devices: none -> 24.6 us  [sent_to_all(): lax.all_to_all(jnp.broadcast_to(value[None], (count, *value.shape)), axis...]
    all_to_all x0 -> x1, starting transfers between devices: none -> 4.29 us  [sent_to_all(): lax.all_to_all(jnp.broadcast_to(value[None], (count, *value.shape)), axis...]
where the time goes in v1:
time: 377 us
  waiting for transfers between devices  213 us (56%)
  blocking collectives  117 us (31%)
  starting transfers between devices  15.2 us (4%)
  between operations  14.1 us (4%)
  matrix products  12.5 us (3%)
  local copies, waits for them, and re-layouts  4.88 us (1%)
    all_gather x2, waiting for transfers between devices, whole_of(): nearer = lax.all_gather(value, axes[-1], axis=dim, tiled=True)  136 us
    all_to_all x1, blocking collectives, shards(): lax.all_to_all(jnp.stack([deviation_block.astype(jnp.bfloat16)] * lax.axi...  59.9 us
    all_to_all x1, blocking collectives, sent_to_all(): lax.all_to_all(jnp.broadcast_to(value[None], (count, *value.shape)), axis...  57.1 us
    all_to_all x1, waiting for transfers between devices, sum_at_owner(): lax.all_to_all(blocks, axis, split_axis=0, concat_axis=0, tiled=True)  51.7 us
    all_to_all x1, waiting for transfers between devices, sent_to_all(): lax.all_to_all(jnp.broadcast_to(value[None], (count, *value.shape)), axis...  24.6 us
    all_to_all x1, starting transfers between devices, sum_at_owner(): lax.all_to_all(blocks, axis, split_axis=0, concat_axis=0, tiled=True)  10.8 us
  transfers between devices with their start and end apart: 4, of which 4 were waited for; matrix products, arithmetic and copies ran while one was open for 0% of the time, Pallas kernels for 0%

profile of v1, /device:TPU:1, one launch (start us, length us, event | category | flops | bytes accessed | tf_op | source)
XLA Modules:
  0.0 376.7 jit_solution(6160965195413190843)
XLA Ops:
  7.2 0.0 all-gather.3.cloned.1.call-start
  7.2 0.7 all-gather.3.cloned.1.call-update
  7.9 0.0 all-gather.5.cloned.1.call-start
  7.9 36.7 %all-gather.3.cloned.1.call-done = bf16[1024,512]{1,0:T(8,128)(2,1)} async-done(((bf16[1024,256]{1,0:T(8,128)(2,1)}), bf16[1024,512]{1,0:T(8,128)(2,1)}) %all-gather.3.cloned.1.call-update) | async-done | bytes 1048592 | tf_op jit(solution)/shard_map/all_gather | solution.py:13
  44.7 0.0 all-gather.5.cloned.1.call-update
  44.7 98.9 %all-gather.5.cloned.1.call-done = bf16[1024,4096]{1,0:T(8,128)(2,1)} async-done(((bf16[1024,512]{1,0:T(8,128)(2,1)}), bf16[1024,4096]{1,0:T(8,128)(2,1)}) %all-gather.5.cloned.1.call-update) | async-done | bytes 8388624 | tf_op jit(solution)/shard_map/all_gather | solution.py:13
  143.6 6.0 %fusion = bf16[32,32,8,128]{3,2,1,0:T(8,128)(2,1)S(1)} fusion(bf16[1024,256]{1,0:T(8,128)(2,1)} %param.1, bf16[1024,4096]{1,0:T(8,128)(2,1)} %all-gather.5.cloned.1.call-done), kind=kOutput, calls=%fused_computation.3 | convolution fusion | flops 2148532224 | bytes 11010048 | tf_op jit(solution)/shard_map/dot_general | solution.py:60
  149.6 1.9 copy.13
  151.5 10.8 %all-to-all-start = ((bf16[32,256,128]{2,1,0:T(8,128)(2,1)}), bf16[32,256,128]{2,1,0:T(8,128)(2,1)S(1)}, u32[]{:S(2)}, u32[]{:S(2)}) async-start(bf16[32,256,128]{2,1,0:T(8,128)(2,1)} %bitcast.23), calls=%async_computation | async-start | bytes 4194304 | tf_op jit(solution)/shard_map/all_to_all | solution.py:24
  162.3 51.7 %all-to-all-done = bf16[32,256,128]{2,1,0:T(8,128)(2,1)S(1)} async-done(((bf16[32,256,128]{2,1,0:T(8,128)(2,1)}), bf16[32,256,128]{2,1,0:T(8,128)(2,1)S(1)}, u32[]{:S(2)}, u32[]{:S(2)}) %all-to-all-start) | async-done | bytes 2097184 | tf_op jit(solution)/shard_map/all_to_all | solution.py:24
  214.0 0.3 convert_reduce_fusion
  214.3 0.1 fusion.4
  214.4 0.0 copy-start
  214.5 1.3 broadcast_in_dim.4
  215.7 4.3 %all-to-all-start.2 = ((bf16[16,256,128]{2,1,0:T(8,128)(2,1)}), bf16[16,256,128]{2,1,0:T(8,128)(2,1)S(1)}, u32[]{:S(2)}, u32[]{:S(2)}) async-start(bf16[16,256,128]{2,1,0:T(8,128)(2,1)} %broadcast_in_dim.4), calls=%async_computation.2 | async-start | bytes 2097152 | tf_op jit(solution)/shard_map/all_to_all | solution.py:36
  220.0 0.1 copy.8
  220.1 24.6 %all-to-all-done.2 = bf16[16,256,128]{2,1,0:T(8,128)(2,1)S(1)} async-done(((bf16[16,256,128]{2,1,0:T(8,128)(2,1)}), bf16[16,256,128]{2,1,0:T(8,128)(2,1)S(1)}, u32[]{:S(2)}, u32[]{:S(2)}) %all-to-all-start.2) | async-done | bytes 1048608 | tf_op jit(solution)/shard_map/all_to_all | solution.py:36
  244.8 0.2 stack.2
  245.0 59.9 %all_to_all.20 = bf16[32,256,128]{1,2,0:T(8,128)(2,1)S(1)} all-to-all(bf16[32,256,128]{1,2,0:T(8,128)(2,1)S(1)} %stack.2), channel_id=1, replica_groups=mesh['band_0'=8,'band_1'=2,'ga'=32] {'ga'}, dimensions={0} | all-to-all | bytes 4194304 | tf_op jit(solution)/shard_map/all_to_all | solution.py:67
  304.9 0.0 copy-done
  304.9 0.8 fusion.3
  305.6 0.1 copy.9
  305.7 0.2 broadcast_in_dim.5
  306.0 57.1 %all_to_all.21 = bf16[32,256,128]{1,2,0:T(8,128)(2,1)S(1)} all-to-all(bf16[32,256,128]{1,2,0:T(8,128)(2,1)S(1)} %broadcast_in_dim.5), channel_id=1, replica_groups=mesh['band_0'=8,'band_1'=2,'ga'=32] {'ga'}, dimensions={0} | all-to-all | bytes 4194304 | tf_op jit(solution)/shard_map/all_to_all | solution.py:36
  363.1 5.8 %fusion.1 = bf16[1024,256]{0,1:T(8,128)(2,1)S(1)} fusion(bf16[256,4096]{0,1:T(8,128)(2,1)S(1)} %bitcast.26, bf16[1024,4096]{1,0:T(8,128)(2,1)} %all-gather.5.cloned.1.call-done), kind=kOutput, calls=%fused_computation.5 | convolution fusion | flops 2147745792 | bytes 11010048 | tf_op jit(solution)/shard_map/dot_general | solution.py:83
  368.8 1.0 copy.10
  (2 shorter events, 0.0 us)
Async XLA Ops:
  7.2 37.5 %all-gather.3.cloned.1.call-start = ((), (), s32[]{:S(2)}) async-start(), calls=%async_computation.4 | async-start | bytes 1572864 | tf_op jit(solution)/shard_map/all_gather | solution.py:13
  7.9 135.7 %all-gather.5.cloned.1.call-start = ((), (), s32[]{:S(2)}) async-start(), calls=%async_computation.5 | async-start | bytes 9437184 | tf_op jit(solution)/shard_map/all_gather | solution.py:13
  151.5 62.5 %all-to-all-start = ((bf16[32,256,128]{2,1,0:T(8,128)(2,1)}), bf16[32,256,128]{2,1,0:T(8,128)(2,1)S(1)}, u32[]{:S(2)}, u32[]{:S(2)}) async-start(bf16[32,256,128]{2,1,0:T(8,128)(2,1)} %bitcast.23), calls=%async_computation | async-start | bytes 4194304 | tf_op jit(solution)/shard_map/all_to_all | solution.py:24
  214.4 90.4 %copy-start = (f32[256,128]{1,0:T(8,128)}, f32[256,128]{1,0:T(8,128)S(1)}, u32[]{:S(2)}) copy-start(f32[256,128]{1,0:T(8,128)S(1)} %get-tuple-element.9) | copy-start | bytes 393220
  215.7 29.0 %all-to-all-start.2 = ((bf16[16,256,128]{2,1,0:T(8,128)(2,1)}), bf16[16,256,128]{2,1,0:T(8,128)(2,1)S(1)}, u32[]{:S(2)}, u32[]{:S(2)}) async-start(bf16[16,256,128]{2,1,0:T(8,128)(2,1)} %broadcast_in_dim.4), calls=%async_computation.2 | async-start | bytes 2097152 | tf_op jit(solution)/shard_map/all_to_all | solution.py:36
Sparse Core Ops, SparseCore 0:
  10.0 34.5 all-gather.2
  46.8 96.7 all-gather.4
